TPU v7x, 32 devices: a whole 2x2x4 slice. The times are simulated.
32 devices in a mesh: row: 8 (over z, core), col: 4 (over y, x).
Axes of the slice: x: 2, y: 2, z: 4, core: 2. Of those that a mesh axis runs over, the one named last changes fastest.
Arguments:
- act_codes: int32 [512, 7168], P('col', 'row'), may hold values from -127 to 127
- act_scales: float32 [512, 112], P('col', 'row'), may hold values from 0.005 to 0.03
- gate_weight: bfloat16 [7168, 18432], P('row', 'col'), may hold values from -0.0625 to 0.0625
- up_weight: bfloat16 [7168, 18432], P('row', 'col'), may hold values from -0.0625 to 0.0625
- down_weight: bfloat16 [18432, 7168], P('col', 'row'), may hold values from -0.046875 to 0.046875
Outputs:
- mixed: bfloat16 [512, 7168], P('col', 'row')
All inputs are finite; a program needn't handle non-finite values.
Results may differ from a plain program's by a relative error of at most 0.03.
Values may be sent and summed in bfloat16 or wider, within the bound.
A program may use at most 128 MiB of HBM per device.

v0:
```python
import jax
import jax.numpy as jnp
from jax import lax
from jax.sharding import PartitionSpec as P


def on_device(act_codes, act_scales, gate_weight, up_weight, down_weight):
    local_rows = act_codes.shape[0]
    width = act_codes.shape[1]
    nblocks = act_scales.shape[1]
    blocked = act_codes.astype(jnp.float32).reshape(local_rows, nblocks, width // nblocks)
    acts = (blocked * act_scales[:, :, None]).reshape(local_rows, width).astype(jnp.bfloat16)
    every = lax.all_gather(acts, "col", axis=0, tiled=True)
    hidden_width = gate_weight.shape[1]
    gate_part = jnp.dot(every, gate_weight, preferred_element_type=jnp.float32)
    up_part = jnp.dot(every, up_weight, preferred_element_type=jnp.float32)
    summed = lax.psum_scatter(
        jnp.concatenate([gate_part, up_part], axis=1).astype(jnp.bfloat16),
        "row",
        scatter_dimension=0,
        tiled=True,
    ).astype(jnp.float32)
    hidden = (jax.nn.silu(summed[:, :hidden_width]) * summed[:, hidden_width:]).astype(jnp.bfloat16)
    partial_value = jnp.dot(
        lax.all_gather(hidden, "row", axis=0, tiled=True),
        down_weight,
        preferred_element_type=jnp.float32,
    )
    mixed = lax.psum_scatter(
        partial_value.astype(jnp.bfloat16), "col", scatter_dimension=0, tiled=True
    )
    return mixed


def solution(mesh):
    placed = (P("col", "row"), P("col", "row"), P("row", "col"), P("row", "col"), P("col", "row"))
    return jax.shard_map(
        on_device, mesh=mesh, in_specs=placed, out_specs=P("col", "row"), check_vma=False
    )
```

profile of v0, /device:TPU:0, one launch (start us, length us, event | category | flops | bytes accessed | tf_op | source)
XLA Modules:
  0.0 236.7 jit_solution(11513722934624598675)
XLA Ops:
  6.5 0.0 reduce-scatter.3.cloned.1.call-start
  6.5 1.2 copy.7
  7.8 0.7 fusion.1
  8.5 0.0 slice-start
  8.5 14.2 %all_gather.6 = bf16[512,896]{0,1:T(8,128)(2,1)S(1)} all-gather(bf16[128,896]{0,1:T(8,128)(2,1)S(1)} %fusion.1), channel_id=1, replica_groups=mesh['row'=8,'col'=4] {'col'}, dimensions={0}, use_global_device_ids=true | all-gather | bytes 1146880 | tf_op jit(solution)/shard_map/all_gather | solution.py:13
  22.7 0.0 slice-start.1
  22.7 8.8 %convolution_convert_fusion = bf16[512,4608]{1,0:T(8,128)(2,1)S(1)} fusion(bf16[512,896]{0,1:T(8,128)(2,1)S(1)} %all_gather.6, bf16[896,4608]{1,0:T(8,128)(2,1)} %param.8), kind=kOutput, calls=%fused_computation.1 | convolution fusion | flops 4230217728 | bytes 13893632 | tf_op jit(solution)/shard_map/dot_general | solution.py:16
  31.5 0.0 slice-done
  31.5 0.0 slice-done.1
  31.6 5.4 %convolution_convert_fusion.1 = bf16[512,4608]{1,0:T(8,128)(2,1)S(1)} fusion(bf16[512,896]{0,1:T(8,128)(2,1)S(1)} %all_gather.6, bf16[896,4608]{1,0:T(8,128)(2,1)S(1)} %bitcast.11), kind=kOutput, calls=%fused_computation.2 | convolution fusion | flops 4230217728 | bytes 13893632 | tf_op jit(solution)/shard_map/dot_general | solution.py:15
  37.0 4.8 %pad_maximum_fusion = bf16[512,9216]{1,0:T(8,128)(2,1)} fusion(bf16[512,4608]{1,0:T(8,128)(2,1)S(1)} %convolution_convert_fusion, bf16[512,4608]{1,0:T(8,128)(2,1)S(1)} %convolution_convert_fusion.1), kind=kLoop, calls=%fused_computation | loop fusion | flops 18874368 | bytes 18874368 | tf_op jit(solution)/shard_map/concatenate | solution.py:18
  41.8 0.0 reduce-scatter.3.cloned.1.call-update
  41.8 0.0 all-gather.2.cloned.1.call-start
  41.9 99.8 %reduce-scatter.3.cloned.1.call-done = bf16[64,9216]{1,0:T(8,128)(2,1)} async-done(((bf16[512,9216]{1,0:T(8,128)(2,1)}), bf16[64,9216]{1,0:T(8,128)(2,1)}) %reduce-scatter.3.cloned.1.call-update) | async-done | bytes 1179664 | tf_op jit(solution)/shard_map/reduce_scatter | solution.py:17
  141.7 1.4 convert_element_type.18
  143.1 1.2 fusion
  144.3 0.0 all-gather.2.cloned.1.call-update
  144.3 0.0 reduce-scatter.5.cloned.1.call-start
  144.3 49.8 %all-gather.2.cloned.1.call-done = bf16[512,4608]{1,0:T(8,128)(2,1)} async-done(((bf16[64,4608]{1,0:T(8,128)(2,1)}), bf16[512,4608]{1,0:T(8,128)(2,1)}) %all-gather.2.cloned.1.call-update) | async-done | bytes 4718608 | tf_op jit(solution)/shard_map/all_gather | solution.py:25
  194.1 10.1 %convolution_convert_fusion.2 = bf16[512,896]{1,0:T(8,128)(2,1)} fusion(bf16[512,4608]{1,0:T(8,128)(2,1)} %all-gather.2.cloned.1.call-done, bf16[4608,896]{1,0:T(8,128)(2,1)} %param.9), kind=kOutput, calls=%fused_computation.3 | convolution fusion | flops 4228317184 | bytes 13893632 | tf_op jit(solution)/shard_map/dot_general | solution.py:24
  204.2 0.0 reduce-scatter.5.cloned.1.call-update
  204.2 26.0 %reduce-scatter.5.cloned.1.call-done = bf16[128,896]{1,0:T(8,128)(2,1)} async-done(((bf16[512,896]{1,0:T(8,128)(2,1)}), bf16[128,896]{1,0:T(8,128)(2,1)}) %reduce-scatter.5.cloned.1.call-update) | async-done | bytes 229392 | tf_op jit(solution)/shard_map/reduce_scatter | solution.py:29
  (1 shorter events, 0.0 us)
Async XLA Ops:
  6.5 135.2 %reduce-scatter.3.cloned.1.call-start = ((), (), s32[]{:S(2)}) async-start(), calls=%async_computation.2 | async-start | bytes 10616832 | tf_op jit(solution)/shard_map/reduce_scatter | solution.py:17
  8.5 23.0 %slice-start = ((s8[8257536]{0:T(1024)(128)(4,1)}), s8[4194304]{0:T(1024)(128)(4,1)S(1)}, s32[]{:S(2)}) async-start(s8[8257536]{0:T(1024)(128)(4,1)} %bitcast.10), calls=%async_computation.5 | async-start | bytes 8388608
  22.7 8.8 %slice-start.1 = ((s8[8257536]{0:T(1024)(128)(4,1)}), s8[4063232]{0:T(1024)(128)(4,1)S(1)}, s32[]{:S(2)}) async-start(s8[8257536]{0:T(1024)(128)(4,1)} %bitcast.10), calls=%async_computation.6 | async-start | bytes 8126464
  41.8 152.3 %all-gather.2.cloned.1.call-start = ((), (), s32[]{:S(2)}) async-start(), calls=%async_computation.3 | async-start | bytes 5308416 | tf_op jit(solution)/shard_map/all_gather | solution.py:25
  144.3 85.9 %reduce-scatter.5.cloned.1.call-start = ((), (), s32[]{:S(2)}) async-start(), calls=%async_computation.4 | async-start | bytes 1146880 | tf_op jit(solution)/shard_map/reduce_scatter | solution.py:29
Sparse Core Ops, SparseCore 0:
  41.9 99.7 reduce-scatter.2
  144.4 49.6 all-gather.1
  204.4 25.8 reduce-scatter.4
where the time goes:
time: 237 us
  waiting for transfers between devices  176 us (74%)
  matrix products  24.3 us (10%)
  blocking collectives  14.2 us (6%)
  between operations  13.2 us (6%)
  other arithmetic  8.09 us (3%)
    reduce_scatter x1, waiting for transfers between devices, on_device(): lax.psum_scatter(jnp.concatenate([gate_part, up_part], axis=1).astype(jnp...  99.8 us
    all_gather x1, waiting for transfers between devices, on_device(): lax.all_gather(hidden, 'row', axis=0, tiled=True)  49.8 us
    reduce_scatter x1, waiting for transfers between devices, on_device(): lax.psum_scatter(partial_value.astype(jnp.bfloat16), 'col', scatter_dimen...  26 us
    all_gather x1, blocking collectives, on_device(): every = lax.all_gather(acts, 'col', axis=0, tiled=True)  14.2 us
    dot_general x1, matrix products, on_device(): jnp.dot(lax.all_gather(hidden, 'row', axis=0, tiled=True), down_weight, p...  10.1 us
    dot_general x1, matrix products, on_device(): up_part = jnp.dot(every, up_weight, preferred_element_type=jnp.float32)  8.82 us
    dot_general x1, matrix products, on_device(): gate_part = jnp.dot(every, gate_weight, preferred_element_type=jnp.float32)  5.45 us
    concatenate x1, other arithmetic, on_device(): jnp.concatenate([gate_part, up_part], axis=1).astype(jnp.bfloat16)  4.77 us
  transfers between devices with their start and end apart: 3, of which 3 were waited for; matrix products, arithmetic and copies ran while one was open for 0% of the time, Pallas kernels for 0%

commit v1 on v0

--- a/solution.py
+++ b/solution.py
@@ -10,7 +10,12 @@
     nblocks = act_scales.shape[1]
     blocked = act_codes.astype(jnp.float32).reshape(local_rows, nblocks, width // nblocks)
     acts = (blocked * act_scales[:, :, None]).reshape(local_rows, width).astype(jnp.bfloat16)
-    every = lax.all_gather(acts, "col", axis=0, tiled=True)
+    ring = [acts]
+    for hop in range(3):
+        ring.append(lax.ppermute(ring[-1], "col", [(dev, (dev + 1) % 4) for dev in range(4)]))
+    every = jnp.roll(
+        jnp.concatenate(ring[::-1], axis=0), (lax.axis_index("col") + 1) * ring[0].shape[0], axis=0
+    )
     hidden_width = gate_weight.shape[1]
     gate_part = jnp.dot(every, gate_weight, preferred_element_type=jnp.float32)
     up_part = jnp.dot(every, up_weight, preferred_element_type=jnp.float32)

time: 237 us -> 248 us (1.046)
  waiting for transfers between devices: 176 us -> 196 us
  blocking collectives: 14.2 us -> 0 us
  starting transfers between devices: 0.09 us -> 3.89 us
    ppermute x0 -> x3, waiting for transfers between devices: none -> 20.4 us  [on_device(): lax.ppermute(ring[-1], 'col', [(dev, (dev + 1) % 4) for dev in range(4)])]
    all_gather x1 -> x0, blocking collectives: 14.2 us -> none  [on_device(): every = lax.all_gather(acts, 'col', axis=0, tiled=True)]
    ppermute x0 -> x3, starting transfers between devices: none -> 3.81 us  [on_device(): lax.ppermute(ring[-1], 'col', [(dev, (dev + 1) % 4) for dev in range(4)])]
  transfers between devices with their start and end apart: 3 -> 6, of which waited for: 3 -> 6; matrix products, arithmetic and copies ran while one was open for 0% -> 0% of each run, Pallas kernels for 0% -> 0%
where the time goes in v1:
time: 248 us; the launch traced here: 247 us
  waiting for transfers between devices  196 us (79%)
  matrix products  24.4 us (10%)
  between operations  13.2 us (5%)
  other arithmetic  8.14 us (3%)
  starting transfers between devices  3.89 us (2%)
    reduce_scatter x1, waiting for transfers between devices, on_device(): lax.psum_scatter(jnp.concatenate([gate_part, up_part], axis=1).astype(jnp...  99.8 us
    all_gather x1, waiting for transfers between devices, on_device(): lax.all_gather(hidden, 'row', axis=0, tiled=True)  49.8 us
    reduce_scatter x1, waiting for transfers between devices, on_device(): lax.psum_scatter(partial_value.astype(jnp.bfloat16), 'col', scatter_dimen...  26 us
    ppermute x3, waiting for transfers between devices, on_device(): lax.ppermute(ring[-1], 'col', [(dev, (dev + 1) % 4) for dev in range(4)])  20.4 us
    dot_general x1, matrix products, on_device(): jnp.dot(lax.all_gather(hidden, 'row', axis=0, tiled=True), down_weight, p...  10.1 us
    dot_general x1, matrix products, on_device(): up_part = jnp.dot(every, up_weight, preferred_element_type=jnp.float32)  8.85 us
    dot_general x1, matrix products, on_device(): gate_part = jnp.dot(every, gate_weight, preferred_element_type=jnp.float32)  5.48 us
  transfers between devices with their start and end apart: 6, of which 6 were waited for; matrix products, arithmetic and copies ran while one was open for 0% of the time, Pallas kernels for 0%

profile of v1, /device:TPU:0, one launch (start us, length us, event | category | flops | bytes accessed | tf_op | source)
XLA Modules:
  0.0 247.4 jit_solution(10797811361236191859)
XLA Ops:
  6.5 1.2 copy.7
  7.8 0.7 fusion.3
  8.5 3.0 %collective-permute-start = (bf16[128,896]{0,1:T(8,128)(2,1)S(1)}, bf16[128,896]{0,1:T(8,128)(2,1)S(1)}, u32[]{:S(2)}, u32[]{:S(2)}) collective-permute-start(bf16[128,896]{0,1:T(8,128)(2,1)S(1)} %fusion.3), channel_id=1, source_target_pairs={{0,1},{1,2},{2,3},{3,0},{4,5},{5,6},{6,7},{7,4},{8,9},{9,10},{10,1... | collective-permute-start | bytes 688136 | tf_op jit(solution)/shard_map/ppermute | solution.py:15
  11.5 6.6 %collective-permute-done = bf16[128,896]{0,1:T(8,128)(2,1)S(1)} collective-permute-done((bf16[128,896]{0,1:T(8,128)(2,1)S(1)}, bf16[128,896]{0,1:T(8,128)(2,1)S(1)}, u32[]{:S(2)}, u32[]{:S(2)}) %collective-permute-start) | collective-permute-done | bytes 229408 | tf_op jit(solution)/shard_map/ppermute | solution.py:15
  18.1 0.8 collective-permute-start.1
  18.9 6.9 %collective-permute-done.1 = bf16[128,896]{0,1:T(8,128)(2,1)S(1)} collective-permute-done((bf16[128,896]{0,1:T(8,128)(2,1)S(1)}, bf16[128,896]{0,1:T(8,128)(2,1)S(1)}, u32[]{:S(2)}, u32[]{:S(2)}) %collective-permute-start.1) | collective-permute-done | bytes 229408 | tf_op jit(solution)/shard_map/ppermute | solution.py:15
  25.8 6.9 %collective-permute-done.2 = bf16[128,896]{0,1:T(8,128)(2,1)S(1)} collective-permute-done((bf16[128,896]{0,1:T(8,128)(2,1)S(1)}, bf16[128,896]{0,1:T(8,128)(2,1)S(1)}, u32[]{:S(2)}, u32[]{:S(2)}) %collective-permute-start.2) | collective-permute-done | bytes 229408 | tf_op jit(solution)/shard_map/ppermute | solution.py:15
  32.7 0.1 constant_dynamic-update-slice_fusion.7
  32.7 0.1 constant_dynamic-update-slice_fusion.6
  32.8 0.1 constant_dynamic-update-slice_fusion.5
  32.9 0.1 constant_dynamic-update-slice_fusion.4
  33.0 0.1 constant_dynamic-update-slice_fusion.3
  33.1 0.1 constant_dynamic-update-slice_fusion.2
  33.1 0.1 constant_dynamic-update-slice_fusion.1
  33.2 0.1 constant_dynamic-update-slice_fusion
  33.3 8.9 %convolution_convert_fusion = bf16[512,4608]{1,0:T(8,128)(2,1)S(1)} fusion(bf16[896,4608]{1,0:T(8,128)(2,1)} %param.8, bf16[1024,896]{0,1:T(8,128)(2,1)S(1)} %constant_dynamic-update-slice_fusion, s32[]{:T(128)S(6)} %select_n.14), kind=kOutput, calls=%fused_computation.1 | convolution fusion | flops 4230217728 | bytes 13893636 | tf_op jit(solution)/shard_map/dot_general | solution.py:21
  42.2 5.5 %convolution_convert_fusion.1 = bf16[512,4608]{1,0:T(8,128)(2,1)S(1)} fusion(bf16[896,4608]{1,0:T(8,128)(2,1)S(1)} %bitcast.9, bf16[1024,896]{0,1:T(8,128)(2,1)S(1)} %constant_dynamic-update-slice_fusion, s32[]{:T(128)S(6)} %select_n.14), kind=kOutput, calls=%fused_computation.2 | convolution fusion | flops 4230217728 | bytes 13893636 | tf_op jit(solution)/shard_map/dot_general | solution.py:20
  47.7 4.8 %pad_maximum_fusion = bf16[512,9216]{1,0:T(8,128)(2,1)} fusion(bf16[512,4608]{1,0:T(8,128)(2,1)S(1)} %convolution_convert_fusion, bf16[512,4608]{1,0:T(8,128)(2,1)S(1)} %convolution_convert_fusion.1), kind=kLoop, calls=%fused_computation | loop fusion | flops 18874368 | bytes 18874368 | tf_op jit(solution)/shard_map/concatenate | solution.py:23
  52.6 99.8 %reduce-scatter.3.cloned.1.call-done = bf16[64,9216]{1,0:T(8,128)(2,1)} async-done(((bf16[512,9216]{1,0:T(8,128)(2,1)}), bf16[64,9216]{1,0:T(8,128)(2,1)}) %reduce-scatter.3.cloned.1.call-update) | async-done | bytes 1179664 | tf_op jit(solution)/shard_map/reduce_scatter | solution.py:22
  152.4 1.4 convert_element_type.18
  153.8 1.2 fusion
  155.0 49.8 %all-gather.2.cloned.1.call-done = bf16[512,4608]{1,0:T(8,128)(2,1)} async-done(((bf16[64,4608]{1,0:T(8,128)(2,1)}), bf16[512,4608]{1,0:T(8,128)(2,1)}) %all-gather.2.cloned.1.call-update) | async-done | bytes 4718608 | tf_op jit(solution)/shard_map/all_gather | solution.py:30
  204.8 10.1 %convolution_convert_fusion.2 = bf16[512,896]{1,0:T(8,128)(2,1)} fusion(bf16[512,4608]{1,0:T(8,128)(2,1)} %all-gather.2.cloned.1.call-done, bf16[4608,896]{1,0:T(8,128)(2,1)} %param.9), kind=kOutput, calls=%fused_computation.3 | convolution fusion | flops 4228317184 | bytes 13893632 | tf_op jit(solution)/shard_map/dot_general | solution.py:29
  214.9 26.0 %reduce-scatter.5.cloned.1.call-done = bf16[128,896]{1,0:T(8,128)(2,1)} async-done(((bf16[512,896]{1,0:T(8,128)(2,1)}), bf16[128,896]{1,0:T(8,128)(2,1)}) %reduce-scatter.5.cloned.1.call-update) | async-done | bytes 229392 | tf_op jit(solution)/shard_map/reduce_scatter | solution.py:34
  (12 shorter events, 0.2 us)
Async XLA Ops:
  6.5 145.8 %reduce-scatter.3.cloned.1.call-start = ((), (), s32[]{:S(2)}) async-start(), calls=%async_computation.2 | async-start | bytes 10616832 | tf_op jit(solution)/shard_map/reduce_scatter | solution.py:22
  8.5 9.6 %collective-permute-start = (bf16[128,896]{0,1:T(8,128)(2,1)S(1)}, bf16[128,896]{0,1:T(8,128)(2,1)S(1)}, u32[]{:S(2)}, u32[]{:S(2)}) collective-permute-start(bf16[128,896]{0,1:T(8,128)(2,1)S(1)} %fusion.3), channel_id=1, source_target_pairs={{0,1},{1,2},{2,3},{3,0},{4,5},{5,6},{6,7},{7,4},{8,9},{9,10},{10,1... | collective-permute-start | bytes 688136 | tf_op jit(solution)/shard_map/ppermute | solution.py:15
  18.1 7.7 %collective-permute-start.1 = (bf16[128,896]{0,1:T(8,128)(2,1)S(1)}, bf16[128,896]{0,1:T(8,128)(2,1)S(1)}, u32[]{:S(2)}, u32[]{:S(2)}) collective-permute-start(bf16[128,896]{0,1:T(8,128)(2,1)S(1)} %collective-permute-done), channel_id=1, source_target_pairs={{0,1},{1,2},{2,3},{3,0},{4,5},{5,6},{6,7},{7,4},{8,9},{9,10},{10,1... | collective-permute-start | bytes 688136 | tf_op jit(solution)/shard_map/ppermute | solution.py:15
  25.8 6.9 %collective-permute-start.2 = (bf16[128,896]{0,1:T(8,128)(2,1)S(1)}, bf16[128,896]{0,1:T(8,128)(2,1)S(1)}, u32[]{:S(2)}, u32[]{:S(2)}) collective-permute-start(bf16[128,896]{0,1:T(8,128)(2,1)S(1)} %collective-permute-done.1), channel_id=1, source_target_pairs={{0,1},{1,2},{2,3},{3,0},{4,5},{5,6},{6,7},{7,4},{8,9},{9,10},{10,1... | collective-permute-start | bytes 688136 | tf_op jit(solution)/shard_map/ppermute | solution.py:15
  33.2 9.0 %slice-start = ((s8[8257536]{0:T(1024)(128)(4,1)}), s8[4194304]{0:T(1024)(128)(4,1)S(1)}, s32[]{:S(2)}) async-start(s8[8257536]{0:T(1024)(128)(4,1)} %bitcast.8), calls=%async_computation.5 | async-start | bytes 8388608
  33.3 8.9 %slice-start.1 = ((s8[8257536]{0:T(1024)(128)(4,1)}), s8[4063232]{0:T(1024)(128)(4,1)S(1)}, s32[]{:S(2)}) async-start(s8[8257536]{0:T(1024)(128)(4,1)} %bitcast.8), calls=%async_computation.6 | async-start | bytes 8126464
  52.5 152.2 %all-gather.2.cloned.1.call-start = ((), (), s32[]{:S(2)}) async-start(), calls=%async_computation.3 | async-start | bytes 5308416 | tf_op jit(solution)/shard_map/all_gather | solution.py:30
  155.0 85.9 %reduce-scatter.5.cloned.1.call-start = ((), (), s32[]{:S(2)}) async-start(), calls=%async_computation.4 | async-start | bytes 1146880 | tf_op jit(solution)/shard_map/reduce_scatter | solution.py:34
Sparse Core Ops, SparseCore 0:
  52.7 99.6 reduce-scatter.2
  155.1 49.6 all-gather.1
  215.0 25.8 reduce-scatter.4
